TPU v7x, 32 devices: a whole 2x2x4 slice. The times are simulated.
32 devices in a mesh: groups: 2 (over x), seq: 8 (over z, y), head: 2 (over core).
Axes of the slice: x: 2, y: 2, z: 4, core: 2. Of those that a mesh axis runs over, the one named last changes fastest.
Arguments:
- q_latent: bfloat16 [16, 64, 512], P(('groups', 'seq'), 'head'), parts along dimension 0, may hold values from -7.5 to 7.5
- q_rope: bfloat16 [16, 4096], P(('groups', 'seq'), 'head'), parts along dimension 0, may hold values from -7.5 to 7.5
- cache_latent: bfloat16 [768, 64, 512], P(('groups', 'seq', 'head')), parts along dimension 0, may hold values from -10 to 10
- cache_rope: bfloat16 [768, 4096], P(('groups', 'seq', 'head')), parts along dimension 0, may hold values from -6 to 6
- page_table: int32 [16, 48], P('groups'), parts along dimension 0, may hold values from 0 to 383, as said below
- lengths: int32 [16], P('groups'), parts along dimension 0, may hold values from 1 to 3072, 14745 in all
Outputs:
- attended: bfloat16 [16, 64, 512], P(('groups', 'seq'), 'head'), parts along dimension 0
There are 2 independent parts, one for each index of `groups`. A program takes and returns all parts, laid end to end along the dimension named above; each array names one. Nothing has to cross between parts.
Inputs may be any that keep to these rules, and one draw needn't show every extreme that they name: `page_table`: device d of a group (d = seq index * 2 + head index) holds pool pages d * 24 to (d + 1) * 24 - 1. Each pool page is named exactly once. A request's logical pages k * 3 to (k + 1) * 3 - 1 lie on one device, and every device holds exactly one such run of every request. `lengths`: the newest token is counted.
All inputs are finite; a program needn't handle non-finite values.
Results may differ from a plain program's by a relative error of at most 0.0055.
Values may be sent and summed in bfloat16 or wider, within the bound.
A program may use at most 128 MiB of HBM per device.

v0:
```python
import math
import jax
import jax.numpy as jnp
from jax import lax
from jax.sharding import PartitionSpec as P

ROPE = 64
NOPE = 128
MASKED_SCORE = -1e30


def softmax_update(carried, query_lat, query_rot, key_rows, rotary, live_mask, score_scale):
    row_max, row_total, summed = carried
    scores = jnp.einsum("hd,td->ht", query_lat, key_rows, preferred_element_type=jnp.float32)
    scores = (
        scores + jnp.einsum("hd,td->ht", query_rot, rotary, preferred_element_type=jnp.float32)
    ) * score_scale
    scores = jnp.where(live_mask[None, :], scores, MASKED_SCORE)
    new_max = jnp.maximum(row_max, jnp.max(scores, axis=1))
    exp_terms = jnp.where(live_mask[None, :], jnp.exp(scores - new_max[:, None]), 0.0)
    weights = exp_terms.astype(jnp.bfloat16)
    summed = jnp.dot(weights, key_rows, preferred_element_type=jnp.float32)
    return (new_max, jnp.sum(exp_terms, axis=1), summed)


def local(q_latent, q_rope, cache_latent, cache_rope, page_table, lengths):
    seq_count = lax.axis_size("seq")
    head_count = lax.axis_size("head")
    my_seq = lax.axis_index("seq")
    my_core = lax.axis_index("head")
    my_device = my_seq * head_count + my_core
    pool_pages, page_len, latent_width = cache_latent.shape
    rope_width = cache_rope.shape[1] // page_len
    request_count, page_slots = page_table.shape
    device_count = seq_count * head_count
    run_len = page_slots // device_count
    run_owner = page_table[:, ::run_len] // pool_pages
    device_ids = jnp.arange(device_count, dtype=jnp.int32)
    run_index = jnp.sum(jnp.where(run_owner == my_device, device_ids[None, :], 0), axis=1)
    offsets = jnp.arange(run_len, dtype=jnp.int32)
    slot_cols = run_index[:, None] * run_len + offsets[None, :]
    local_slots = jnp.take_along_axis(page_table, slot_cols, axis=1) - my_device * pool_pages
    flat_slots = local_slots.reshape(-1)
    picked_lat = cache_latent[flat_slots].reshape(request_count, run_len, page_len, latent_width)
    picked_rot = cache_rope[flat_slots].reshape(request_count, run_len, page_len * rope_width)
    score_scale = 1.0 / math.sqrt(NOPE + ROPE)
    token_ids = jnp.arange(page_len, dtype=jnp.int32)
    arrived = (
        lax.all_to_all(picked_lat, "seq", split_axis=0, concat_axis=1, tiled=True),
        lax.all_to_all(picked_rot, "seq", split_axis=0, concat_axis=1, tiled=True),
    )
    own_length = lengths[my_seq]
    own_owner = run_owner[my_seq]
    run_of_device = jnp.sum(
        jnp.where(own_owner[None, :] == device_ids[:, None], device_ids[None, :], 0), axis=1
    )
    heads_here = q_latent.shape[1]
    query_lat = q_latent[0]
    query_rot = q_rope[0].reshape(heads_here, rope_width)
    per_core = seq_count * run_len
    start_carry = (
        jnp.full((heads_here,), MASKED_SCORE, jnp.float32),
        jnp.zeros((heads_here,), jnp.float32),
        jnp.zeros((heads_here, latent_width), jnp.float32),
    )
    piece_lat = lax.all_gather(arrived[0], "head", axis=1, tiled=True)
    piece_rot = lax.all_gather(arrived[1], "head", axis=1, tiled=True)
    piece_count = piece_lat.shape[1]
    gathered = jnp.arange(piece_count, dtype=jnp.int32)
    source_core = gathered // per_core
    within = gathered % per_core
    source = within // run_len * head_count + source_core
    page_start = (run_of_device[source] * run_len + within % run_len) * page_len
    positions = (page_start[:, None] + token_ids[None, :]).reshape(-1)
    live_mask = positions < own_length
    key_rows = piece_lat.reshape(piece_count * page_len, latent_width)
    rotary = piece_rot.reshape(piece_count * page_len, rope_width)
    row_max, row_total, summed = softmax_update(
        start_carry, query_lat, query_rot, key_rows, rotary, live_mask, score_scale
    )
    return (summed / row_total[:, None]).astype(jnp.bfloat16)[None]


def solution(mesh):
    return jax.shard_map(
        local,
        mesh=mesh,
        in_specs=(
            P(("groups", "seq"), "head", None),
            P(("groups", "seq"), "head"),
            P(("groups", "seq", "head"), None, None),
            P(("groups", "seq", "head"), None),
            P("groups", None),
            P("groups"),
        ),
        out_specs=P(("groups", "seq"), "head", None),
        check_vma=False,
    )
```

profile of v0, /device:TPU:0, one launch (start us, length us, event | category | flops | bytes accessed | tf_op | source)
XLA Modules:
  0.0 83.4 jit_solution(11498527822076780127)
XLA Ops:
  6.5 0.0 copy-start
  6.5 0.0 all-gather.2.cloned.1.call-start
  6.5 0.9 %slice.3 = s32[8,16]{1,0:T(8,128)S(1)} slice(s32[8,48]{1,0:T(8,128)} %param.10), slice={[0:8:1], [0:48:3]} | slice | bytes 1024 | tf_op jit(solution)/shard_map/slice | solution.py:37
  7.4 0.1 select_reduce_fusion.1
  7.6 0.1 fusion.13
  7.6 0.1 reshape.281
  7.7 1.5 %gather_fusion.3 = s32[24]{0:T(128)S(1)} fusion(s32[8,48]{1,0:T(8,128)} %param.10, s32[24]{0:T(128)S(1)} %reshape.281), kind=kCustom, calls=%fused_computation.3 | custom fusion | bytes 384 | tf_op jit(solution)/shard_map/jit(take_along_axis)/gather | solution.py:42
  9.2 0.1 add.189
  9.3 0.1 add.190
  9.4 0.1 add.192
  9.5 0.0 copy-done
  9.5 0.6 gather_fusion.1
  10.2 0.0 copy-start.2
  10.2 0.0 copy-start.5
  10.2 44.3 %all_to_all.24 = bf16[8,3,64,512]{3,2,1,0:T(8,128)(2,1)} all-to-all(bf16[8,3,64,512]{3,2,1,0:T(8,128)(2,1)S(1)} %bitcast.34), channel_id=1, replica_groups=mesh['groups'=2,'seq'=8,'head'=2] {'seq'}, dimensions={0} | all-to-all | bytes 3145728 | tf_op jit(solution)/shard_map/all_to_all | solution.py:49
  54.5 0.0 copy-start.4
  54.5 0.0 all-gather.2.cloned.1.call-update
  54.6 0.0 copy-done.2
  54.6 0.0 copy-start.3
  54.6 0.7 gather_fusion.2
  55.3 0.8 %reshape.255 = bf16[8,3,4096]{2,1,0:T(4,128)(2,1)} reshape(bf16[24,4096]{1,0:T(8,128)(2,1)S(1)} %gather_fusion.2) | data formatting | bytes 393216 | tf_op jit(solution)/shard_map/reshape | solution.py:45
  56.1 3.6 %all-to-all-start.1 = ((bf16[8,3,4096]{2,1,0:T(4,128)(2,1)}), bf16[8,3,4096]{2,1,0:T(4,128)(2,1)S(1)}, u32[]{:S(2)}, u32[]{:S(2)}) async-start(bf16[8,3,4096]{2,1,0:T(4,128)(2,1)} %reshape.255), calls=%async_computation.1 | async-start | bytes 524288 | tf_op jit(solution)/shard_map/all_to_all | solution.py:50
  59.7 0.0 copy-done.5
  59.7 0.6 dynamic_slice.7
  60.3 0.1 select_reduce_fusion
  60.5 0.8 gather_fusion
  61.3 0.7 add_compare_fusion
  62.0 0.1 lt.81
  62.1 0.0 copy-done.4
  62.1 0.1 reshape_squeeze.3
  62.2 6.1 %all-to-all-done.1 = bf16[8,3,4096]{2,1,0:T(4,128)(2,1)S(1)} async-done(((bf16[8,3,4096]{2,1,0:T(4,128)(2,1)}), bf16[8,3,4096]{2,1,0:T(4,128)(2,1)S(1)}, u32[]{:S(2)}, u32[]{:S(2)}) %all-to-all-start.1) | async-done | bytes 196640 | tf_op jit(solution)/shard_map/all_to_all | solution.py:50
  68.3 0.2 all_to_all.21
  68.4 2.1 %all_gather.7 = bf16[1,48,4096]{2,1,0:T(8,128)(2,1)S(1)} all-gather(bf16[1,24,4096]{2,1,0:T(8,128)(2,1)S(1)} %all_to_all.21), channel_id=1, replica_groups=mesh['groups'=2,'seq'=8,'head'=2] {'head'}, dimensions={1}, use_global_device_ids=true | all-gather | bytes 589824 | tf_op jit(solution)/shard_map/all_gather | solution.py:67
  70.5 0.8 %reshape.256 = bf16[3072,64]{1,0:T(8,128)(2,1)S(1)} reshape(bf16[1,48,4096]{2,1,0:T(8,128)(2,1)S(1)} %all_gather.7) | data formatting | bytes 786432 | tf_op jit(solution)/shard_map/reshape | solution.py:77
  71.4 0.4 fusion.23
  71.7 0.0 all-gather.2.cloned.1.call-done
  71.7 0.0 copy-done.3
  71.7 0.0 copy-start.1
  71.8 3.2 %fusion.22 = (f32[32]{0:T(128)S(1)}, f32[3072,32]{0,1:T(8,128)S(1)}) fusion(f32[3072,32]{0,1:T(8,128)S(1)} %fusion.23, bf16[3072,512]{1,0:T(8,128)(2,1)} %bitcast.31, bf16[1,32,512]{2,1,0:T(8,128)(2,1)S(1)} %copy-done.3, pred[3072]{0:T(1024)(128)(4,1)S(1)} %lt.81), kind=kOutput, calls=%fused_computation.53 | convolution fusion | flops 101056480 | bytes 3968128 | tf_op jit(solution)/shard_map/hd,td->ht/dot_general | solution.py:14
  75.0 0.3 fusion.4
  75.2 0.0 copy-done.1
  75.2 1.3 %fusion.3 = bf16[1,32,512]{2,1,0:T(8,128)(2,1)} fusion(bf16[3072,512]{1,0:T(8,128)(2,1)S(1)} %bitcast.32, f32[3072,32]{0,1:T(8,128)S(1)} %get-tuple-element.8, f32[32]{0:T(128)S(1)} %broadcast_maximum_fusion, pred[3072]{0:T(1024)(128)(4,1)S(1)} %lt.81, f32[32]{0:T(128)S(1)} %fusion.4), kind=kOutput, calls=%fused_computation.9 | convolution fusion | flops 100990976 | bytes 3575040 | tf_op jit(solution)/shard_map/dot_general | solution.py:22
  (10 shorter events, 0.1 us)
Async XLA Ops:
  6.5 3.0 %copy-start = (bf16[24,64,512]{2,1,0:T(8,128)(2,1)S(1)}, bf16[24,64,512]{2,1,0:T(8,128)(2,1)}, u32[]{:S(2)}) copy-start(bf16[24,64,512]{2,1,0:T(8,128)(2,1)} %param.8) | copy-start | bytes 4718596
  6.5 65.2 %all-gather.2.cloned.1.call-start = ((), (), s32[]{:S(2)}) async-start(), calls=%async_computation.2 | async-start | bytes 4718592 | tf_op jit(solution)/shard_map/all_gather | solution.py:66
  10.2 44.4 %copy-start.2 = (bf16[24,4096]{1,0:T(8,128)(2,1)S(1)}, bf16[24,4096]{1,0:T(8,128)(2,1)}, u32[]{:S(2)}) copy-start(bf16[24,4096]{1,0:T(8,128)(2,1)} %param.9) | copy-start | bytes 589828
  10.2 49.5 %copy-start.5 = (s32[8]{0:T(128)S(1)}, s32[8]{0:T(128)}, u32[]{:S(2)}) copy-start(s32[8]{0:T(128)} %param.11) | copy-start | bytes 100
  54.5 7.5 %copy-start.4 = (bf16[1,2048]{1,0:T(2,128)(2,1)S(1)}, bf16[1,2048]{1,0:T(2,128)(2,1)}, u32[]{:S(2)}) copy-start(bf16[1,2048]{1,0:T(2,128)(2,1)} %param.7) | copy-start | bytes 12292
  54.6 17.2 %copy-start.3 = (bf16[1,32,512]{2,1,0:T(8,128)(2,1)S(1)}, bf16[1,32,512]{2,1,0:T(8,128)(2,1)}, u32[]{:S(2)}) copy-start(bf16[1,32,512]{2,1,0:T(8,128)(2,1)} %param.6) | copy-start | bytes 98308
  56.1 12.2 %all-to-all-start.1 = ((bf16[8,3,4096]{2,1,0:T(4,128)(2,1)}), bf16[8,3,4096]{2,1,0:T(4,128)(2,1)S(1)}, u32[]{:S(2)}, u32[]{:S(2)}) async-start(bf16[8,3,4096]{2,1,0:T(4,128)(2,1)} %reshape.255), calls=%async_computation.1 | async-start | bytes 524288 | tf_op jit(solution)/shard_map/all_to_all | solution.py:50
  71.7 3.5 %copy-start.1 = (bf16[1,48,64,512]{3,2,0,1:T(8,128)(2,1)S(1)}, bf16[1,48,64,512]{3,2,0,1:T(8,128)(2,1)}, u32[]{:S(2)}) copy-start(bf16[1,48,64,512]{3,2,0,1:T(8,128)(2,1)} %all-gather.2.cloned.1.call-done) | copy-start | bytes 9437188
Sparse Core Ops, SparseCore 0:
  54.7 11.1 all-gather.1
where the time goes:
time: 83.7 us; the launch traced here: 83.4 us
  blocking collectives  46.4 us (55%)
  between operations  13.6 us (16%)
  local copies, waits for them, and re-layouts  7.45 us (9%)
  waiting for transfers between devices  6.07 us (7%)
  matrix products  4.85 us (6%)
  starting transfers between devices  3.6 us (4%)
  other arithmetic  1.42 us (2%)
    all_to_all x1, blocking collectives, local(): lax.all_to_all(picked_lat, 'seq', split_axis=0, concat_axis=1, tiled=True)  44.3 us
    all_to_all x1, waiting for transfers between devices, local(): lax.all_to_all(picked_rot, 'seq', split_axis=0, concat_axis=1, tiled=True)  6.05 us
    all_to_all x1, starting transfers between devices, local(): lax.all_to_all(picked_rot, 'seq', split_axis=0, concat_axis=1, tiled=True)  3.59 us
    dot_general x1, matrix products, softmax_update(): jnp.einsum('hd,td->ht', query_lat, key_rows, preferred_element_type=jnp.f...  3.18 us
    all_gather x1, blocking collectives, local(): piece_rot = lax.all_gather(arrived[1], 'head', axis=1, tiled=True)  2.09 us
  transfers between devices with their start and end apart: 2, of which 1 were waited for; matrix products, arithmetic and copies ran while one was open for 6% of the time, Pallas kernels for 0%

commit v1 on v0

--- a/solution.py
+++ b/solution.py
@@ -7,6 +7,28 @@
 ROPE = 64
 NOPE = 128
 MASKED_SCORE = -1e30
+
+
+def cut_along(value, dim, size):
+    before, after = (value.shape[:dim], value.shape[dim + 1 :])
+    return jnp.moveaxis(value.reshape(*before, size, -1, *after), dim, 0)
+
+
+def in_order(blocks, dim):
+    blocks = jnp.moveaxis(blocks, 0, dim)
+    shape = blocks.shape
+    return blocks.reshape(*shape[:dim], shape[dim] * shape[dim + 1], *shape[dim + 2 :])
+
+
+def exchange_directly(x, axis, split_dim, concat_dim):
+    count, index = (lax.axis_size(axis), lax.axis_index(axis))
+    blocks = cut_along(x, split_dim, count)
+    done = [blocks[index]]
+    for step in range(1, count):
+        sent = blocks[(index + step) % count]
+        done.append(lax.ppermute(sent, axis, [(i, (i + step) % count) for i in range(count)]))
+    blocks = jnp.stack(done)[(index - jnp.arange(count)) % count]
+    return in_order(blocks, concat_dim)
 
 
 def softmax_update(carried, query_lat, query_rot, key_rows, rotary, live_mask, score_scale):
@@ -47,7 +69,7 @@
     token_ids = jnp.arange(page_len, dtype=jnp.int32)
     arrived = (
         lax.all_to_all(picked_lat, "seq", split_axis=0, concat_axis=1, tiled=True),
-        lax.all_to_all(picked_rot, "seq", split_axis=0, concat_axis=1, tiled=True),
+        exchange_directly(picked_rot, "seq", 0, 1),
     )
     own_length = lengths[my_seq]
     own_owner = run_owner[my_seq]

time: 83.7 us -> 88.1 us (1.053)
  blocking collectives: 46.4 us -> 2.09 us
  waiting for transfers between devices: 6.07 us -> 30.6 us
  starting transfers between devices: 3.6 us -> 17 us
  local copies, waits for them, and re-layouts: 7.45 us -> 18.1 us
    all_to_all x1 -> x0, blocking collectives: 44.3 us -> none  [local(): lax.all_to_all(picked_lat, 'seq', split_axis=0, concat_axis=1, tiled=True)]
    ppermute x0 -> x7, waiting for transfers between devices: none -> 24.9 us  [exchange_directly(): lax.ppermute(sent, axis, [(i, (i + step) % count) for i in range(count)])]
    ppermute x0 -> x7, starting transfers between devices: none -> 9.54 us  [exchange_directly(): lax.ppermute(sent, axis, [(i, (i + step) % count) for i in range(count)])]
    all_to_all x1, waiting for transfers between devices: 6.05 us -> 0.01 us  [local(): lax.all_to_all(picked_lat, 'seq', split_axis=0, concat_axis=1, tiled=True)]
    all_gather x1, waiting for transfers between devices: 0.01 us -> 5.66 us  [local(): piece_lat = lax.all_gather(arrived[0], 'head', axis=1, tiled=True)]
    unnamed x12 -> x18, local copies, waits for them, and re-layouts: 0.04 us -> 4.86 us
    all_to_all x1, starting transfers between devices: 3.59 us -> 7.44 us  [local(): lax.all_to_all(picked_lat, 'seq', split_axis=0, concat_axis=1, tiled=True)]
    another operation x0 -> x3, local copies, waits for them, and re-layouts: none -> 1.84 us  [the longest x1 1.05 us: cut_along(): return jnp.moveaxis(value.reshape(*before, size, -1, *after), dim, 0)]
  transfers between devices with their start and end apart: 2 -> 9, of which waited for: 1 -> 3; matrix products, arithmetic and copies ran while one was open for 6% -> 16% of each run, Pallas kernels for 0% -> 0%
where the time goes in v1:
time: 88.1 us; the launch traced here: 87.8 us
  waiting for transfers between devices  30.6 us (35%)
  local copies, waits for them, and re-layouts  18.1 us (21%)
  starting transfers between devices  17 us (19%)
  between operations  13.7 us (16%)
  matrix products  4.85 us (6%)
  blocking collectives  2.09 us (2%)
  other arithmetic  1.41 us (2%)
    ppermute x7, waiting for transfers between devices, exchange_directly(): lax.ppermute(sent, axis, [(i, (i + step) % count) for i in range(count)])  24.9 us
    ppermute x7, starting transfers between devices, exchange_directly(): lax.ppermute(sent, axis, [(i, (i + step) % count) for i in range(count)])  9.54 us
    all_to_all x1, starting transfers between devices, local(): lax.all_to_all(picked_lat, 'seq', split_axis=0, concat_axis=1, tiled=True)  7.44 us
    all_gather x1, waiting for transfers between devices, local(): piece_lat = lax.all_gather(arrived[0], 'head', axis=1, tiled=True)  5.66 us
    unnamed x18, local copies, waits for them, and re-layouts  4.86 us
    dot_general x1, matrix products, softmax_update(): jnp.einsum('hd,td->ht', query_lat, key_rows, preferred_element_type=jnp.f...  3.18 us
    all_gather x1, blocking collectives, local(): piece_rot = lax.all_gather(arrived[1], 'head', axis=1, tiled=True)  2.09 us
    gather x1, local copies, waits for them, and re-layouts, local(): cache_latent[flat_slots]  1.85 us
  transfers between devices with their start and end apart: 9, of which 3 were waited for; matrix products, arithmetic and copies ran while one was open for 16% of the time, Pallas kernels for 0%

profile of v1, /device:TPU:0, one launch (start us, length us, event | category | flops | bytes accessed | tf_op | source)
XLA Modules:
  0.0 87.8 jit_solution(15224345042897603496)
XLA Ops:
  6.5 0.0 copy-start
  6.6 0.9 %slice.3 = s32[8,16]{1,0:T(8,128)S(1)} slice(s32[8,48]{1,0:T(8,128)} %param.10), slice={[0:8:1], [0:48:3]} | slice | bytes 1024 | tf_op jit(solution)/shard_map/slice | solution.py:59
  7.5 0.1 select_reduce_fusion.1
  7.6 0.1 fusion.13
  7.7 0.1 reshape.333
  7.8 1.5 %gather_fusion.4 = s32[24]{0:T(128)S(1)} fusion(s32[8,48]{1,0:T(8,128)} %param.10, s32[24]{0:T(128)S(1)} %reshape.333), kind=kCustom, calls=%fused_computation.4 | custom fusion | bytes 384 | tf_op jit(solution)/shard_map/jit(take_along_axis)/gather | solution.py:64
  9.3 0.1 add.277
  9.3 0.1 add.278
  9.4 0.1 add.280
  9.5 0.0 copy-done
  9.5 0.0 copy-start.2
  9.5 1.8 %gather_fusion.1 = bf16[24,64,512]{2,1,0:T(8,128)(2,1)} fusion(bf16[24,64,512]{2,1,0:T(8,128)(2,1)S(1)} %copy-done, s32[1024]{0:T(1024)S(1)} %get-tuple-element.17), kind=kCustom, calls=%fused_computation.1 | custom fusion | bytes 3145824 | tf_op jit(solution)/shard_map/gather | solution.py:66
  11.4 0.0 copy-start.5
  11.4 7.4 %all-to-all-start = ((bf16[8,3,64,512]{3,2,1,0:T(8,128)(2,1)}), bf16[8,3,64,512]{3,2,1,0:T(8,128)(2,1)S(1)}, u32[]{:S(2)}, u32[]{:S(2)}) async-start(bf16[8,3,64,512]{3,2,1,0:T(8,128)(2,1)} %bitcast.65), calls=%async_computation | async-start | bytes 3145728 | tf_op jit(solution)/shard_map/all_to_all | solution.py:71
  18.8 0.0 all-gather.2.cloned.1.call-start
  19.0 0.0 copy-done.2
  19.0 1.4 %gather_fusion.2 = bf16[24,4096]{1,0:T(8,128)(2,1)} fusion(bf16[24,4096]{1,0:T(8,128)(2,1)S(1)} %copy-done.2, s32[1024]{0:T(1024)S(1)} %get-tuple-element.17), kind=kCustom, calls=%fused_computation.2 | custom fusion | bytes 393312 | tf_op jit(solution)/shard_map/gather | solution.py:67
  20.3 1.1 %reshape_reshape.3 = bf16[8,1,3,4096]{3,2,0,1:T(4,128)(2,1)S(1)} reshape(bf16[24,4096]{1,0:T(8,128)(2,1)} %gather_fusion.2) | data formatting | bytes 393216 | tf_op jit(solution)/shard_map/reshape;reshape | solution.py:14
  21.4 0.7 dynamic-slice_bitcast_fusion
  22.2 1.9 %collective-permute-start = (bf16[1,3,4096]{2,1,0:T(4,128)(2,1)}, bf16[1,3,4096]{2,1,0:T(4,128)(2,1)S(1)}, u32[]{:S(2)}, u32[]{:S(2)}) collective-permute-start(bf16[1,3,4096]{2,1,0:T(4,128)(2,1)} %get-tuple-element.13), channel_id=1, source_target_pairs={{0,2},{2,4},{4,6},{6,8},{8,10},{10,12},{12,14},{14,0},{1,3},{3,5},... | collective-permute-start | bytes 73736 | tf_op jit(solution)/shard_map/ppermute | solution.py:29
  24.1 1.5 %collective-permute-start.1 = (bf16[1,3,4096]{2,1,0:T(4,128)(2,1)}, bf16[1,3,4096]{2,1,0:T(4,128)(2,1)S(1)}, u32[]{:S(2)}, u32[]{:S(2)}) collective-permute-start(bf16[1,3,4096]{2,1,0:T(4,128)(2,1)} %get-tuple-element.12), channel_id=1, source_target_pairs={{0,4},{2,6},{4,8},{6,10},{8,12},{10,14},{12,0},{14,2},{1,5},{3,7},... | collective-permute-start | bytes 73736 | tf_op jit(solution)/shard_map/ppermute | solution.py:29
  25.5 2.4 %collective-permute-start.2 = (bf16[1,3,4096]{2,1,0:T(4,128)(2,1)}, bf16[1,3,4096]{2,1,0:T(4,128)(2,1)S(1)}, u32[]{:S(2)}, u32[]{:S(2)}) collective-permute-start(bf16[1,3,4096]{2,1,0:T(4,128)(2,1)} %get-tuple-element.11), channel_id=1, source_target_pairs={{0,6},{2,8},{4,10},{6,12},{8,14},{10,0},{12,2},{14,4},{1,7},{3,9},... | collective-permute-start | bytes 73736 | tf_op jit(solution)/shard_map/ppermute | solution.py:29
  27.9 1.5 %collective-permute-start.3 = (bf16[1,3,4096]{2,1,0:T(4,128)(2,1)S(1)}, bf16[1,3,4096]{2,1,0:T(4,128)(2,1)S(1)}, u32[]{:S(2)}, u32[]{:S(2)}) collective-permute-start(bf16[1,3,4096]{2,1,0:T(4,128)(2,1)S(1)} %get-tuple-element.10), channel_id=1, source_target_pairs={{0,8},{2,10},{4,12},{6,14},{8,0},{10,2},{12,4},{14,6},{1,9},{3,11}... | collective-permute-start | bytes 73736 | tf_op jit(solution)/shard_map/ppermute | solution.py:29
  29.3 2.4 %collective-permute-start.4 = (bf16[1,3,4096]{2,1,0:T(4,128)(2,1)S(1)}, bf16[1,3,4096]{2,1,0:T(4,128)(2,1)S(1)}, u32[]{:S(2)}, u32[]{:S(2)}) collective-permute-start(bf16[1,3,4096]{2,1,0:T(4,128)(2,1)S(1)} %get-tuple-element.9), channel_id=1, source_target_pairs={{0,10},{2,12},{4,14},{6,0},{8,2},{10,4},{12,6},{14,8},{1,11},{3,13... | collective-permute-start | bytes 73736 | tf_op jit(solution)/shard_map/ppermute | solution.py:29
  31.7 1.3 %dynamic_slice.31 = s32[1]{0:T(128)} dynamic-slice(s32[8]{0:T(128)} %param.11, s32[]{:T(128)S(6)} %select_n.206), dynamic_slice_sizes={1} | dynamic-slice | bytes 12 | tf_op jit(solution)/shard_map/dynamic_slice | solution.py:74
  33.0 0.1 select_reduce_fusion
  33.1 0.8 gather_fusion
  33.9 0.0 copy-start.4
  33.9 0.7 add_compare_fusion
  34.6 0.0 copy-done.5
  34.7 0.1 reshape_squeeze.3
  34.8 0.1 lt.149
  34.9 16.5 %collective-permute-done = bf16[1,3,4096]{2,1,0:T(4,128)(2,1)S(1)} collective-permute-done((bf16[1,3,4096]{2,1,0:T(4,128)(2,1)}, bf16[1,3,4096]{2,1,0:T(4,128)(2,1)S(1)}, u32[]{:S(2)}, u32[]{:S(2)}) %collective-permute-start) | collective-permute-done | bytes 24608 | tf_op jit(solution)/shard_map/ppermute | solution.py:29
  51.4 0.0 collective-permute-start.5
  51.4 0.6 bitcast_dynamic-update-slice_fusion.6
  52.0 0.0 collective-permute-done.1
  52.0 0.0 collective-permute-start.6
  52.0 0.6 bitcast_dynamic-update-slice_fusion.5
  52.6 8.4 %collective-permute-done.2 = bf16[1,3,4096]{2,1,0:T(4,128)(2,1)S(1)} collective-permute-done((bf16[1,3,4096]{2,1,0:T(4,128)(2,1)}, bf16[1,3,4096]{2,1,0:T(4,128)(2,1)S(1)}, u32[]{:S(2)}, u32[]{:S(2)}) %collective-permute-start.2) | collective-permute-done | bytes 24608 | tf_op jit(solution)/shard_map/ppermute | solution.py:29
  61.0 0.6 bitcast_dynamic-update-slice_fusion.4
  61.6 0.0 all-to-all-done
  61.6 0.0 copy-start.3
  61.6 1.1 %copy-done.3 = bf16[8,3,64,512]{3,2,1,0:T(8,128)(2,1)} copy-done((bf16[8,3,64,512]{3,2,1,0:T(8,128)(2,1)}, bf16[8,3,64,512]{3,2,1,0:T(8,128)(2,1)S(1)}, u32[]{:S(2)}) %copy-start.3) | copy-done | bytes 1572888
  62.8 0.0 all-gather.2.cloned.1.call-update
  62.8 0.0 collective-permute-done.3
  62.8 0.6 bitcast_dynamic-update-slice_fusion.3
  63.4 0.0 collective-permute-done.4
  63.4 0.6 bitcast_dynamic-update-slice_fusion.2
  64.1 0.0 collective-permute-done.5
  64.1 0.6 bitcast_dynamic-update-slice_fusion.1
  64.7 0.0 collective-permute-done.6
  64.7 0.6 bitcast_dynamic-update-slice_fusion
  65.3 1.7 %gather_fusion.3 = bf16[8,3,4096]{2,1,0:T(4,128)(2,1)S(1)} fusion(bf16[8,3,4096]{2,1,0:T(4,128)(2,1)} %bitcast.66, s32[1024]{0:T(1024)S(1)} %pad_clamp_fusion), kind=kCustom, calls=%fused_computation.3 | custom fusion | bytes 393248 | tf_op jit(solution)/shard_map/gather | solution.py:30
  67.0 0.2 reshape_transpose.3
  67.2 2.1 %all_gather.7 = bf16[1,48,4096]{2,1,0:T(8,128)(2,1)S(1)} all-gather(bf16[1,24,4096]{2,1,0:T(8,128)(2,1)S(1)} %reshape_transpose.3), channel_id=1, replica_groups=mesh['groups'=2,'seq'=8,'head'=2] {'head'}, dimensions={1}, use_global_device_ids=true | all-gather | bytes 589824 | tf_op jit(solution)/shard_map/all_gather | solution.py:89
  69.3 0.8 reshape.298
  70.1 0.4 fusion.26
  70.5 5.7 %all-gather.2.cloned.1.call-done = bf16[1,48,64,512]{3,2,0,1:T(8,128)(2,1)} async-done(((bf16[1,24,64,512]{3,2,0,1:T(8,128)(2,1)}), bf16[1,48,64,512]{3,2,0,1:T(8,128)(2,1)}) %all-gather.2.cloned.1.call-update) | async-done | bytes 3145744 | tf_op jit(solution)/shard_map/all_gather | solution.py:88
  76.1 0.0 copy-done.4
  76.1 0.0 copy-start.1
  76.1 3.2 %fusion.25 = (f32[32]{0:T(128)S(1)}, f32[3072,32]{0,1:T(8,128)S(1)}) fusion(f32[3072,32]{0,1:T(8,128)S(1)} %fusion.26, bf16[3072,512]{1,0:T(8,128)(2,1)} %bitcast.62, bf16[1,32,512]{2,1,0:T(8,128)(2,1)S(1)} %copy-done.4, pred[3072]{0:T(1024)(128)(4,1)S(1)} %lt.149), kind=kOutput, calls=%fused_computation.77 | convolution fusion | flops 101056480 | bytes 3968128 | tf_op jit(solution)/shard_map/hd,td->ht/dot_general | solution.py:36
  79.3 0.3 fusion.4
  79.6 0.0 copy-done.1
  79.6 1.3 %fusion.3 = bf16[1,32,512]{2,1,0:T(8,128)(2,1)} fusion(bf16[3072,512]{1,0:T(8,128)(2,1)S(1)} %bitcast.63, f32[3072,32]{0,1:T(8,128)S(1)} %get-tuple-element.16, f32[32]{0:T(128)S(1)} %broadcast_maximum_fusion, pred[3072]{0:T(1024)(128)(4,1)S(1)} %lt.149, f32[32]{0:T(128)S(1)} %fusion.4), kind=kOutput, calls=%fused_computation.10 | convolution fusion | flops 100990976 | bytes 3575040 | tf_op jit(solution)/shard_map/dot_general | solution.py:44
  (11 shorter events, 0.1 us)
Async XLA Ops:
  6.5 3.0 %copy-start = (bf16[24,64,512]{2,1,0:T(8,128)(2,1)S(1)}, bf16[24,64,512]{2,1,0:T(8,128)(2,1)}, u32[]{:S(2)}) copy-start(bf16[24,64,512]{2,1,0:T(8,128)(2,1)} %param.8) | copy-start | bytes 4718596
  9.5 9.4 %copy-start.2 = (bf16[24,4096]{1,0:T(8,128)(2,1)S(1)}, bf16[24,4096]{1,0:T(8,128)(2,1)}, u32[]{:S(2)}) copy-start(bf16[24,4096]{1,0:T(8,128)(2,1)} %param.9) | copy-start | bytes 589828
  11.4 23.2 %copy-start.5 = (bf16[1,2048]{1,0:T(2,128)(2,1)S(1)}, bf16[1,2048]{1,0:T(2,128)(2,1)}, u32[]{:S(2)}) copy-start(bf16[1,2048]{1,0:T(2,128)(2,1)} %param.7) | copy-start | bytes 12292
  11.4 50.2 %all-to-all-start = ((bf16[8,3,64,512]{3,2,1,0:T(8,128)(2,1)}), bf16[8,3,64,512]{3,2,1,0:T(8,128)(2,1)S(1)}, u32[]{:S(2)}, u32[]{:S(2)}) async-start(bf16[8,3,64,512]{3,2,1,0:T(8,128)(2,1)} %bitcast.65), calls=%async_computation | async-start | bytes 3145728 | tf_op jit(solution)/shard_map/all_to_all | solution.py:71
  18.8 57.3 %all-gather.2.cloned.1.call-start = ((), (), s32[]{:S(2)}) async-start(), calls=%async_computation.1 | async-start | bytes 4718592 | tf_op jit(solution)/shard_map/all_gather | solution.py:88
  22.2 29.2 %collective-permute-start = (bf16[1,3,4096]{2,1,0:T(4,128)(2,1)}, bf16[1,3,4096]{2,1,0:T(4,128)(2,1)S(1)}, u32[]{:S(2)}, u32[]{:S(2)}) collective-permute-start(bf16[1,3,4096]{2,1,0:T(4,128)(2,1)} %get-tuple-element.13), channel_id=1, source_target_pairs={{0,2},{2,4},{4,6},{6,8},{8,10},{10,12},{12,14},{14,0},{1,3},{3,5},... | collective-permute-start | bytes 73736 | tf_op jit(solution)/shard_map/ppermute | solution.py:29
  24.1 27.9 %collective-permute-start.1 = (bf16[1,3,4096]{2,1,0:T(4,128)(2,1)}, bf16[1,3,4096]{2,1,0:T(4,128)(2,1)S(1)}, u32[]{:S(2)}, u32[]{:S(2)}) collective-permute-start(bf16[1,3,4096]{2,1,0:T(4,128)(2,1)} %get-tuple-element.12), channel_id=1, source_target_pairs={{0,4},{2,6},{4,8},{6,10},{8,12},{10,14},{12,0},{14,2},{1,5},{3,7},... | collective-permute-start | bytes 73736 | tf_op jit(solution)/shard_map/ppermute | solution.py:29
  25.5 35.5 %collective-permute-start.2 = (bf16[1,3,4096]{2,1,0:T(4,128)(2,1)}, bf16[1,3,4096]{2,1,0:T(4,128)(2,1)S(1)}, u32[]{:S(2)}, u32[]{:S(2)}) collective-permute-start(bf16[1,3,4096]{2,1,0:T(4,128)(2,1)} %get-tuple-element.11), channel_id=1, source_target_pairs={{0,6},{2,8},{4,10},{6,12},{8,14},{10,0},{12,2},{14,4},{1,7},{3,9},... | collective-permute-start | bytes 73736 | tf_op jit(solution)/shard_map/ppermute | solution.py:29
  27.9 34.9 %collective-permute-start.3 = (bf16[1,3,4096]{2,1,0:T(4,128)(2,1)S(1)}, bf16[1,3,4096]{2,1,0:T(4,128)(2,1)S(1)}, u32[]{:S(2)}, u32[]{:S(2)}) collective-permute-start(bf16[1,3,4096]{2,1,0:T(4,128)(2,1)S(1)} %get-tuple-element.10), channel_id=1, source_target_pairs={{0,8},{2,10},{4,12},{6,14},{8,0},{10,2},{12,4},{14,6},{1,9},{3,11}... | collective-permute-start | bytes 73736 | tf_op jit(solution)/shard_map/ppermute | solution.py:29
  29.3 34.1 %collective-permute-start.4 = (bf16[1,3,4096]{2,1,0:T(4,128)(2,1)S(1)}, bf16[1,3,4096]{2,1,0:T(4,128)(2,1)S(1)}, u32[]{:S(2)}, u32[]{:S(2)}) collective-permute-start(bf16[1,3,4096]{2,1,0:T(4,128)(2,1)S(1)} %get-tuple-element.9), channel_id=1, source_target_pairs={{0,10},{2,12},{4,14},{6,0},{8,2},{10,4},{12,6},{14,8},{1,11},{3,13... | collective-permute-start | bytes 73736 | tf_op jit(solution)/shard_map/ppermute | solution.py:29
  33.9 42.2 %copy-start.4 = (bf16[1,32,512]{2,1,0:T(8,128)(2,1)S(1)}, bf16[1,32,512]{2,1,0:T(8,128)(2,1)}, u32[]{:S(2)}) copy-start(bf16[1,32,512]{2,1,0:T(8,128)(2,1)} %param.6) | copy-start | bytes 98308
  51.4 12.7 %collective-permute-start.5 = (bf16[1,3,4096]{2,1,0:T(4,128)(2,1)S(1)}, bf16[1,3,4096]{2,1,0:T(4,128)(2,1)S(1)}, u32[]{:S(2)}, u32[]{:S(2)}) collective-permute-start(bf16[1,3,4096]{2,1,0:T(4,128)(2,1)S(1)} %get-tuple-element.8), channel_id=1, source_target_pairs={{0,12},{2,14},{4,0},{6,2},{8,4},{10,6},{12,8},{14,10},{1,13},{3,15... | collective-permute-start | bytes 73736 | tf_op jit(solution)/shard_map/ppermute | solution.py:29
  52.0 12.7 %collective-permute-start.6 = (bf16[1,3,4096]{2,1,0:T(4,128)(2,1)S(1)}, bf16[1,3,4096]{2,1,0:T(4,128)(2,1)S(1)}, u32[]{:S(2)}, u32[]{:S(2)}) collective-permute-start(bf16[1,3,4096]{2,1,0:T(4,128)(2,1)S(1)} %get-tuple-element.7), channel_id=1, source_target_pairs={{0,14},{2,0},{4,2},{6,4},{8,6},{10,8},{12,10},{14,12},{1,15},{3,1}... | collective-permute-start | bytes 73736 | tf_op jit(solution)/shard_map/ppermute | solution.py:29
  61.6 1.2 %copy-start.3 = (bf16[8,3,64,512]{3,2,1,0:T(8,128)(2,1)}, bf16[8,3,64,512]{3,2,1,0:T(8,128)(2,1)S(1)}, u32[]{:S(2)}) copy-start(bf16[8,3,64,512]{3,2,1,0:T(8,128)(2,1)S(1)} %all-to-all-done) | copy-start | bytes 4718596
  76.1 3.5 %copy-start.1 = (bf16[1,48,64,512]{3,2,0,1:T(8,128)(2,1)S(1)}, bf16[1,48,64,512]{3,2,0,1:T(8,128)(2,1)}, u32[]{:S(2)}) copy-start(bf16[1,48,64,512]{3,2,0,1:T(8,128)(2,1)} %all-gather.2.cloned.1.call-done) | copy-start | bytes 9437188
Sparse Core Ops, SparseCore 0:
  62.9 13.1 all-gather.1
